TPU v7x, 32 devices: a whole 2x2x4 slice. The times are simulated.
32 devices in a mesh: span: 8 (over y, x, core), head: 4 (over z).
Axes of the slice: x: 2, y: 2, z: 4, core: 2. Of those that a mesh axis runs over, the one named last changes fastest.
Arguments:
- decoder_states: bfloat16 [16384, 1024], P('span'), may hold values from -21 to 21
- encodings: bfloat16 [512, 128, 1024], P('span', 'head'), may hold values from -21 to 21
- neighbor_table: int32 [256, 2, 2], P('span'), may hold values from 0 to 63, as said below
- query_weight: bfloat16 [1024, 1024], P(None, 'head'), may hold values from -0.1875 to 0.1875
- key_weight: bfloat16 [1024, 1024], P(None, 'head'), may hold values from -0.1875 to 0.1875
- value_weight: bfloat16 [1024, 1024], P(None, 'head'), may hold values from -0.1875 to 0.1875
- out_weight: bfloat16 [1024, 1024], P('head'), may hold values from -0.1875 to 0.1875
Outputs:
- attended: bfloat16 [16384, 1024], P('span', 'head')
Inputs may be any that keep to these rules, and one draw needn't show every extreme that they name: neighbor_table[c, k, 0] is the database shard and neighbor_table[c, k, 1] the slot in that shard of neighbor k of span c; in each aligned block of 32 spans (the spans of one device along `span`) every shard is named by exactly one neighbor, and every slot of every shard is named exactly once in the whole table.
All inputs are finite; a program needn't handle non-finite values.
Results may differ from a plain program's by a relative error of at most 0.012.
The roundings to bfloat16 on the way count: a program that leaves them out, or rounds other values in their place, can miss the bound.
Values may be sent and summed in bfloat16 or wider, within the bound.
A program may use at most 128 MiB of HBM per device.

v0:
```python
import jax
import jax.numpy as jnp
from jax import lax
from jax.sharding import PartitionSpec as P

HEAD_DIM = 64
SPAN_LEN = 64
SEQ_LEN = 2048


def body(
    decoder_states, encodings, neighbor_table, query_weight, key_weight, value_weight, out_weight
):
    peer_count = lax.axis_size("span")
    column_rows = lax.all_to_all(out_weight, "head", split_axis=1, concat_axis=0, tiled=True)
    shard_ids = neighbor_table[:, :, 0].reshape(-1)
    slot_ids = neighbor_table[:, :, 1].reshape(-1)
    entries = shard_ids.shape[0]
    per_peer = entries // peer_count
    numbering = jnp.arange(entries, dtype=jnp.int32)
    same_before = (shard_ids[:, None] == shard_ids[None, :]) & (
        numbering[None, :] < numbering[:, None]
    )
    ranking = jnp.sum(same_before.astype(jnp.int32), axis=1)
    position = shard_ids * per_peer + ranking
    placed = position[None, :] == numbering[:, None]
    request = jnp.sum(jnp.where(placed, slot_ids[None, :], 0), axis=1)
    wanted = lax.all_to_all(request, "span", split_axis=0, concat_axis=0, tiled=True)
    selected = encodings[wanted]
    model_width = decoder_states.shape[1]
    group_cols = query_weight.shape[1]
    both_weights = jnp.concatenate([key_weight, value_weight], axis=1)
    arrived = lax.all_to_all(selected, "span", split_axis=0, concat_axis=0, tiled=True)
    block_in = lax.all_gather(arrived, "head", axis=1, tiled=True)
    flattened = block_in.reshape(-1, model_width)
    result = jnp.dot(flattened, both_weights, preferred_element_type=jnp.float32).astype(
        jnp.bfloat16
    )
    projected = result.reshape(block_in.shape[0], block_in.shape[1], 2 * group_cols)
    ordered = projected[position]
    span_count = neighbor_table.shape[0]
    neighbors = neighbor_table.shape[1]
    heads_here = group_cols // HEAD_DIM
    ordered = ordered.reshape(span_count, neighbors * projected.shape[1], 2 * group_cols)
    key_rows = ordered[:, :, :group_cols].reshape(span_count, -1, heads_here, HEAD_DIM)
    value_rows = ordered[:, :, group_cols:].reshape(span_count, -1, heads_here, HEAD_DIM)
    queries = jnp.dot(decoder_states, query_weight, preferred_element_type=jnp.float32).astype(
        jnp.bfloat16
    )
    sequences = decoder_states.shape[0] // SEQ_LEN
    offset = SPAN_LEN - 1
    queries = queries.reshape(sequences, SEQ_LEN, group_cols)
    shifted = jnp.concatenate(
        [queries[:, offset:], jnp.zeros((sequences, offset, group_cols), jnp.bfloat16)], axis=1
    )
    shifted = shifted.reshape(span_count, SPAN_LEN, heads_here, HEAD_DIM)
    inv_root = HEAD_DIM ** (-0.5)
    scores = (
        jnp.einsum("cqhd,ckhd->chqk", shifted, key_rows, preferred_element_type=jnp.float32)
        * inv_root
    )
    weights = jax.nn.softmax(scores, axis=-1).astype(jnp.bfloat16)
    context = jnp.einsum(
        "chqk,ckhd->cqhd", weights, value_rows, preferred_element_type=jnp.float32
    ).astype(jnp.bfloat16)
    context = context.reshape(sequences, SEQ_LEN, group_cols)
    context = jnp.concatenate(
        [jnp.zeros((sequences, offset, group_cols), jnp.bfloat16), context[:, : SEQ_LEN - offset]],
        axis=1,
    )
    context = context.reshape(-1, group_cols)
    summed = jnp.dot(
        lax.all_gather(context, "head", axis=1, tiled=True),
        column_rows,
        preferred_element_type=jnp.float32,
    )
    return summed.astype(jnp.bfloat16)


def solution(mesh):
    return jax.shard_map(
        body,
        mesh=mesh,
        in_specs=(
            P("span", None),
            P("span", "head", None),
            P("span", None, None),
            P(None, "head"),
            P(None, "head"),
            P(None, "head"),
            P("head", None),
        ),
        out_specs=P("span", "head"),
        check_vma=False,
    )
```

profile of v0, /device:TPU:0, one launch (start us, length us, event | category | flops | bytes accessed | tf_op | source)
XLA Modules:
  0.0 540.0 jit_solution(15045644248357253628)
XLA Ops:
  6.5 0.8 fusion.30
  8.1 9.7 %all_to_all.36 = s32[8,8,1]{1,2,0:T(1,128)S(1)} all-to-all(s32[8,8,1]{1,2,0:T(1,128)S(1)} %bitcast.53), channel_id=1, replica_groups=mesh['span'=8,'head'=4] {'span'}, dimensions={0} | all-to-all | bytes 512 | tf_op jit(solution)/shard_map/all_to_all | solution.py:28
  17.8 0.5 broadcast.71
  18.3 0.7 reduce.3
  19.0 4.9 gather_fusion
  24.0 53.5 %all_to_all.37 = bf16[64,32,1024]{2,1,0:T(8,128)(2,1)} all-to-all(bf16[64,32,1024]{2,1,0:T(8,128)(2,1)} %gather_fusion), channel_id=1, replica_groups=mesh['span'=8,'head'=4] {'span'}, dimensions={0} | all-to-all | bytes 8388608 | tf_op jit(solution)/shard_map/all_to_all | solution.py:33
  77.8 3.4 fusion.11
  81.5 1.0 concatenate.10
  82.5 3.4 reshape.106
  86.0 277.8 %all-gather.4.cloned.1.call-done = bf16[64,128,1024]{2,1,0:T(8,128)(2,1)} async-done(((bf16[64,32,1024]{2,1,0:T(8,128)(2,1)}), bf16[64,128,1024]{2,1,0:T(8,128)(2,1)}) %all-gather.4.cloned.1.call-update) | async-done | bytes 16777232 | tf_op jit(solution)/shard_map/all_gather | solution.py:34
  363.8 14.5 %convolution_convert_fusion = bf16[8192,512]{1,0:T(8,128)(2,1)} fusion(bf16[8192,1024]{1,0:T(8,128)(2,1)} %bitcast.56, bf16[1024,256]{1,0:T(8,128)(2,1)S(1)} %copy-done.4, bf16[1024,256]{1,0:T(8,128)(2,1)} %param.11), kind=kOutput, calls=%fused_computation.3 | convolution fusion | flops 8596226048 | bytes 26214400 | tf_op jit(solution)/shard_map/dot_general | solution.py:36
  378.3 8.9 %gather_fusion.1 = bf16[64,128,512]{2,1,0:T(8,128)(2,1)} fusion(bf16[64,128,512]{2,1,0:T(8,128)(2,1)} %bitcast.47, s32[1024]{0:T(1024)S(1)} %pad_clamp_fusion), kind=kCustom, calls=%fused_computation.1 | custom fusion | bytes 16777472 | tf_op jit(solution)/shard_map/gather | solution.py:40
  387.2 5.9 %fusion.29 = (bf16[32,256,256]{2,1,0:T(8,128)(2,1)}, bf16[32,256,256]{2,1,0:T(8,128)(2,1)}) fusion(bf16[32,256,512]{2,1,0:T(8,128)(2,1)} %bitcast.45), kind=kLoop, calls=%fused_computation.39 | loop fusion | bytes 16777216 | tf_op jit(solution)/shard_map/slice | solution.py:45
  393.1 6.4 %copy.63 = bf16[32,256,256]{1,2,0:T(8,128)(2,1)} copy(bf16[32,256,256]{2,1,0:T(8,128)(2,1)} %get-tuple-element.5) | data formatting | bytes 8388608
  399.5 3.4 fusion.12
  402.9 3.1 fusion.31
  406.2 6.4 %copy.62 = bf16[32,256,256]{1,2,0:T(8,128)(2,1)} copy(bf16[32,256,256]{2,1,0:T(8,128)(2,1)} %get-tuple-element.6) | data formatting | bytes 8388608
  412.5 22.4 %convert_bitcast_fusion = bf16[32,64,4,64]{1,3,2,0:T(8,128)(2,1)} fusion(bf16[32,256,4,64]{1,3,2,0:T(8,128)(2,1)} %bitcast.49, f32[32,4,64]{2,1,0:T(4,128)S(1)} %fusion.31, f32[32,4,64,256]{3,2,1,0:T(8,128)} %copy-done.2), kind=kOutput, calls=%fused_computation.17 | convolution fusion | flops 279453952 | bytes 13664256 | tf_op jit(solution)/shard_map/chqk,ckhd->cqhd/dot_general | solution.py:63
  434.9 2.9 copy.58
  437.9 2.4 reshape.108
  440.3 2.6 concatenate.11
  443.2 30.4 %all_to_all.38 = bf16[256,4,256]{0,2,1:T(8,128)(2,1)S(1)} all-to-all(bf16[256,4,256]{0,2,1:T(8,128)(2,1)S(1)} %bitcast.51), channel_id=1, replica_groups=mesh['span'=8,'head'=4] {'head'}, dimensions={1} | all-to-all | bytes 1048576 | tf_op jit(solution)/shard_map/all_to_all | solution.py:15
  473.8 54.9 %all-gather.6.cloned.1.call-done = bf16[1,2048,1024]{1,2,0:T(8,128)(2,1)} async-done(((bf16[1,2048,256]{1,2,0:T(8,128)(2,1)}), bf16[1,2048,1024]{1,2,0:T(8,128)(2,1)}) %all-gather.6.cloned.1.call-update) | async-done | bytes 4194320 | tf_op jit(solution)/shard_map/all_gather | solution.py:73
  528.6 4.6 fusion.8
  (33 shorter events, 1.9 us)
Async XLA Ops:
  6.5 71.2 %copy-start = (bf16[1024,256]{1,0:T(8,128)(2,1)S(1)}, bf16[1024,256]{1,0:T(8,128)(2,1)}, u32[]{:S(2)}) copy-start(bf16[1024,256]{1,0:T(8,128)(2,1)} %param.10) | copy-start | bytes 1572868
  6.5 357.2 %all-gather.4.cloned.1.call-start = ((), (), s32[]{:S(2)}) async-start(), calls=%async_computation.3 | async-start | bytes 20971520 | tf_op jit(solution)/shard_map/all_gather | solution.py:34
  77.5 451.1 %all-gather.6.cloned.1.call-start = ((), (), s32[]{:S(2)}) async-start(), calls=%async_computation.4 | async-start | bytes 5242880 | tf_op jit(solution)/shard_map/all_gather | solution.py:73
  81.2 282.6 %copy-start.4 = (bf16[1024,256]{1,0:T(8,128)(2,1)S(1)}, bf16[1024,256]{1,0:T(8,128)(2,1)}, u32[]{:S(2)}) copy-start(bf16[1024,256]{1,0:T(8,128)(2,1)} %param.12) | copy-start | bytes 1572868
  402.9 3.2 copy-start.2
  437.9 5.1 copy-start.3
  528.6 4.6 copy-start.1
Sparse Core Ops, SparseCore 0:
  77.6 286.1 all-gather.3
  443.1 85.4 all-gather.5
where the time goes:
time: 541 us; the launch traced here: 540 us
  waiting for transfers between devices  333 us (62%)
  blocking collectives  93.6 us (17%)
  matrix products  48.3 us (9%)
  local copies, waits for them, and re-layouts  47.7 us (9%)
  between operations  13.5 us (2%)
    all_gather x1, waiting for transfers between devices, body(): block_in = lax.all_gather(arrived, 'head', axis=1, tiled=True)  278 us
    all_gather x1, waiting for transfers between devices, body(): lax.all_gather(context, 'head', axis=1, tiled=True)  54.9 us
    all_to_all x1, blocking collectives, body(): lax.all_to_all(selected, 'span', split_axis=0, concat_axis=0, tiled=True)  53.5 us
    all_to_all x1, blocking collectives, body(): lax.all_to_all(out_weight, 'head', split_axis=1, concat_axis=0, tiled=True)  30.4 us
    dot_general x1, matrix products, body(): jnp.einsum('chqk,ckhd->cqhd', weights, value_rows, preferred_element_type...  22.4 us
    dot_general x1, matrix products, body(): jnp.dot(flattened, both_weights, preferred_element_type=jnp.float32)  14.5 us
    unnamed x13, local copies, waits for them, and re-layouts  13.1 us
  transfers between devices with their start and end apart: 2, of which 2 were waited for; matrix products, arithmetic and copies ran while one was open for 2% of the time, Pallas kernels for 0%

commit v1 on v0

v1 whole, which is shorter than its diff:
```python
import functools

import jax
import jax.numpy as jnp
from jax import lax
from jax.experimental import pallas as pl
from jax.experimental.pallas import tpu as pltpu
from jax.sharding import PartitionSpec as P

HEAD_DIM = 64
SPAN_LEN = 64
SEQ_LEN = 2048
VMEM = 56 * 1024 * 1024


def matmul_kernel(x_ref, w_ref, o_ref):
    w = w_ref[...].reshape(x_ref.shape[1], o_ref.shape[1])
    o_ref[...] = jnp.dot(x_ref[...], w, preferred_element_type=jnp.float32).astype(o_ref.dtype)


def grouped_matmul(x, w, cols, col_block, tile):
    peers, groups, depth, _ = w.shape
    rows, width = x.shape
    return pl.pallas_call(
        matmul_kernel,
        out_shape=jax.ShapeDtypeStruct((rows, groups * cols), jnp.bfloat16),
        grid=(groups, rows // tile),
        in_specs=[
            pl.BlockSpec((tile, width), lambda g, i: (i, 0)),
            pl.BlockSpec((peers, 1, depth, cols), lambda g, i: (0, g, 0, col_block)),
        ],
        out_specs=pl.BlockSpec((tile, cols), lambda g, i: (i, g)),
        compiler_params=pltpu.CompilerParams(vmem_limit_bytes=VMEM),
        cost_estimate=pl.CostEstimate(
            flops=2 * rows * width * groups * cols, bytes_accessed=16 << 20, transcendentals=0
        ),
    )(x, w)


def attend_kernel(position_ref, q_ref, kv_ref, ctx_ref, lse_ref, *, spans, neighbors, group_cols):
    step = pl.program_id(0)
    width = q_ref.shape[1]
    heads = width // HEAD_DIM
    packed = group_cols // HEAD_DIM
    tokens = kv_ref.shape[1]
    keys = neighbors * tokens
    wide = packed * keys
    row_head = lax.broadcasted_iota(jnp.int32, (wide, group_cols), 0) // keys
    col_head = lax.broadcasted_iota(jnp.int32, (wide, group_cols), 1) // HEAD_DIM
    diagonal = row_head == col_head
    lane_head = lax.broadcasted_iota(jnp.int32, (SPAN_LEN, wide), 1) // keys
    lse_lane = lax.broadcasted_iota(jnp.int32, (SPAN_LEN, 128), 1)
    lse_rows = []
    for c in range(spans):
        span = step * spans + c
        rows = [kv_ref[position_ref[span * neighbors + k]] for k in range(neighbors)]
        kv = jnp.concatenate(rows, axis=0)
        lse_all = jnp.zeros((SPAN_LEN, 128), jnp.float32)
        for g in range(width // group_cols):
            base = g * 2 * group_cols
            q = q_ref[c * SPAN_LEN : (c + 1) * SPAN_LEN, g * group_cols : (g + 1) * group_cols]
            k = kv[:, base : base + group_cols]
            v = kv[:, base + group_cols : base + 2 * group_cols]
            k_wide = jnp.where(diagonal, jnp.concatenate([k] * packed, axis=0), 0)
            v_wide = jnp.where(diagonal, jnp.concatenate([v] * packed, axis=0), 0)
            s = lax.dot_general(
                q, k_wide, (((1,), (1,)), ((), ())), preferred_element_type=jnp.float32
            ) * (HEAD_DIM ** (-0.5))
            top = jnp.zeros_like(s)
            tops = []
            for n in range(packed):
                m = jnp.max(jnp.where(lane_head == n, s, -jnp.inf), axis=1, keepdims=True)
                tops.append(m)
                top = jnp.where(lane_head == n, m, top)
            e = jnp.exp(s - top)
            inv = jnp.zeros_like(s)
            for n in range(packed):
                l = jnp.sum(jnp.where(lane_head == n, e, 0.0), axis=1, keepdims=True)
                inv = jnp.where(lane_head == n, 1.0 / l, inv)
                lse_all = jnp.where(lse_lane == g * packed + n, tops[n] + jnp.log(l), lse_all)
            p = (e * inv).astype(jnp.bfloat16)
            out = jnp.dot(p, v_wide, preferred_element_type=jnp.float32)
            ctx_ref[c * SPAN_LEN : (c + 1) * SPAN_LEN, g * group_cols : (g + 1) * group_cols] = (
                out.astype(ctx_ref.dtype)
            )
        lse_rows.append(lse_all)
    lse_ref[...] = jnp.concatenate(lse_rows, axis=0).T[:heads]


def attend(position, q, kv, span_count, neighbors, group_cols, spans=2):
    rows, width = q.shape
    heads = width // HEAD_DIM
    entries, tokens, wide = kv.shape
    return pl.pallas_call(
        functools.partial(
            attend_kernel, spans=spans, neighbors=neighbors, group_cols=group_cols
        ),
        out_shape=(
            jax.ShapeDtypeStruct((rows, width), jnp.bfloat16),
            jax.ShapeDtypeStruct((heads, rows), jnp.float32),
        ),
        grid_spec=pltpu.PrefetchScalarGridSpec(
            num_scalar_prefetch=1,
            grid=(span_count // spans,),
            in_specs=[
                pl.BlockSpec((spans * SPAN_LEN, width), lambda i, p: (i, 0)),
                pl.BlockSpec((entries, tokens, wide), lambda i, p: (0, 0, 0)),
            ],
            out_specs=[
                pl.BlockSpec((spans * SPAN_LEN, width), lambda i, p: (i, 0)),
                pl.BlockSpec((heads, spans * SPAN_LEN), lambda i, p: (0, i)),
            ],
        ),
        compiler_params=pltpu.CompilerParams(vmem_limit_bytes=VMEM),
        cost_estimate=pl.CostEstimate(
            flops=2 << 32, bytes_accessed=16 << 20, transcendentals=1 << 21
        ),
    )(position, q, kv)


def project_kernel(ctx_ref, own_ref, all_ref, w_ref, o_ref):
    own = own_ref[...]
    every = all_ref[...]
    top = jnp.max(every, axis=0)
    total = jnp.sum(jnp.exp(every - top[None]), axis=0)
    scale = jnp.exp(own - top) / total
    high = scale.astype(jnp.bfloat16)
    low = (scale - high.astype(jnp.float32)).astype(jnp.bfloat16)
    heads = scale.shape[0]
    width = ctx_ref.shape[1]
    spread = (
        lax.broadcasted_iota(jnp.int32, (2 * heads, width), 0) % heads
        == lax.broadcasted_iota(jnp.int32, (2 * heads, width), 1) // HEAD_DIM
    ).astype(jnp.bfloat16)
    factor = lax.dot_general(
        jnp.concatenate([high, low], axis=0),
        spread,
        (((0,), (0,)), ((), ())),
        preferred_element_type=jnp.float32,
    )
    scaled = (ctx_ref[...].astype(jnp.float32) * factor).astype(jnp.bfloat16)
    o_ref[...] = jnp.dot(scaled, w_ref[...], preferred_element_type=jnp.float32).astype(
        o_ref.dtype
    )


def project(ctx, own, every, w, tile=512):
    rows, width = ctx.shape
    groups, heads, _ = every.shape
    return pl.pallas_call(
        project_kernel,
        out_shape=jax.ShapeDtypeStruct((rows, w.shape[1]), jnp.bfloat16),
        grid=(rows // tile,),
        in_specs=[
            pl.BlockSpec((tile, width), lambda i: (i, 0)),
            pl.BlockSpec((heads, tile), lambda i: (0, i)),
            pl.BlockSpec((groups, heads, tile), lambda i: (0, 0, i)),
            pl.BlockSpec(w.shape, lambda i: (0, 0)),
        ],
        out_specs=pl.BlockSpec((tile, w.shape[1]), lambda i: (i, 0)),
        compiler_params=pltpu.CompilerParams(vmem_limit_bytes=VMEM),
    )(ctx, own, every, w)


def body(
    decoder_states, encodings, neighbor_table, query_weight, key_weight, value_weight, out_weight
):
    peer_count = lax.axis_size("span")
    groups = lax.axis_size("head")
    model_width = decoder_states.shape[1]
    group_cols = query_weight.shape[1]
    me = lax.axis_index("span")
    packed = jnp.concatenate([key_weight, value_weight, query_weight], axis=1)
    part = model_width // peer_count
    packed = lax.dynamic_slice_in_dim(packed, me * part, part, 0)
    gathered = lax.all_gather(packed, ("span", "head"), axis=0, tiled=False)
    gathered = gathered.reshape(peer_count, groups, part, 3 * group_cols)
    out_part = group_cols // peer_count
    out_slice = lax.dynamic_slice_in_dim(out_weight, me * out_part, out_part, 0)
    out_all = lax.all_gather(out_slice, ("head", "span"), axis=0, tiled=True)

    shard_ids = neighbor_table[:, :, 0].reshape(-1)
    slot_ids = neighbor_table[:, :, 1].reshape(-1)
    entries = shard_ids.shape[0]
    per_peer = entries // peer_count
    numbering = jnp.arange(entries, dtype=jnp.int32)
    same_before = (shard_ids[:, None] == shard_ids[None, :]) & (
        numbering[None, :] < numbering[:, None]
    )
    ranking = jnp.sum(same_before.astype(jnp.int32), axis=1)
    position = shard_ids * per_peer + ranking
    placed = position[None, :] == numbering[:, None]
    request = jnp.sum(jnp.where(placed, slot_ids[None, :], 0), axis=1)
    wanted = lax.all_to_all(request, "span", split_axis=0, concat_axis=0, tiled=True)
    selected = encodings[wanted]
    arrived = lax.all_to_all(selected, "span", split_axis=0, concat_axis=0, tiled=True)

    sequences = decoder_states.shape[0] // SEQ_LEN
    offset = SPAN_LEN - 1
    states = decoder_states.reshape(sequences, SEQ_LEN, model_width)
    states = jnp.concatenate(
        [states[:, offset:], jnp.zeros((sequences, offset, model_width), states.dtype)], axis=1
    ).reshape(-1, model_width)
    tile = min(1024, decoder_states.shape[0])
    queries = grouped_matmul(states, gathered, group_cols, 2, tile)
    kv = grouped_matmul(arrived.reshape(-1, model_width), gathered, 2 * group_cols, 0, tile)
    kv = kv.reshape(entries, arrived.shape[1], -1)
    context, lse = attend(
        position, queries, kv, neighbor_table.shape[0], neighbor_table.shape[1], group_cols
    )
    every = lax.all_gather(lse, "head", axis=0, tiled=False)
    partial = project(context, lse, every, out_all)
    summed = lax.psum_scatter(partial, "head", scatter_dimension=1, tiled=True)
    summed = summed.reshape(sequences, SEQ_LEN, -1)
    summed = jnp.concatenate(
        [jnp.zeros((sequences, offset, summed.shape[2]), summed.dtype), summed[:, :-offset]], axis=1
    )
    return summed.reshape(decoder_states.shape[0], -1)


def solution(mesh):
    return jax.shard_map(
        body,
        mesh=mesh,
        in_specs=(
            P("span", None),
            P("span", "head", None),
            P("span", None, None),
            P(None, "head"),
            P(None, "head"),
            P(None, "head"),
            P("head", None),
        ),
        out_specs=P("span", "head"),
        check_vma=False,
    )
```

time: 541 us -> 303 us (0.56)
  waiting for transfers between devices: 333 us -> 142 us
  Pallas kernels: 0 us -> 97.3 us
  blocking collectives: 93.6 us -> 26.4 us
  matrix products: 48.3 us -> 0 us
  local copies, waits for them, and re-layouts: 47.7 us -> 15.7 us
    all_gather x2, waiting for transfers between devices: 333 us -> 62.2 us  [the longest x1 62.2 us: body(): gathered = lax.all_gather(packed, ('span', 'head'), axis=0, tiled=False)]
    pallas_call x0 -> x4, Pallas kernels: none -> 97.3 us  [the longest x1 59 us: attend(): pl.pallas_call(functools.partial(attend_kernel, spans=spans, neighbors=ne...]
    all_to_all x2 -> x0, blocking collectives: 83.9 us -> none  [the longest x1 53.5 us: body(): lax.all_to_all(selected, 'span', split_axis=0, concat_axis=0, tiled=True)]
    reduce_scatter x0 -> x1, waiting for transfers between devices: none -> 80 us  [body(): summed = lax.psum_scatter(partial, 'head', scatter_dimension=1, tiled=True)]
    dot_general x5 -> x0, matrix products: 48.3 us -> none  [the longest x1 22.4 us: body(): jnp.einsum('chqk,ckhd->cqhd', weights, value_rows, preferred_element_type...]
    all_gather x0 -> x1, blocking collectives: none -> 16.7 us  [body(): every = lax.all_gather(lse, 'head', axis=0, tiled=False)]
    unnamed x13 -> x4, local copies, waits for them, and re-layouts: 13.1 us -> 0.01 us
    gather x1 -> x0, local copies, waits for them, and re-layouts: 8.91 us -> none  [body(): ordered = projected[position]]
  transfers between devices with their start and end apart: 2 -> 4, of which waited for: 2 -> 2; matrix products, arithmetic and copies ran while one was open for 2% -> 5% of each run, Pallas kernels for 0% -> 29%
where the time goes in v1:
time: 303 us; the launch traced here: 302 us
  waiting for transfers between devices  142 us (47%)
  Pallas kernels  97.3 us (32%)
  blocking collectives  26.4 us (9%)
  local copies, waits for them, and re-layouts  15.7 us (5%)
  between operations  13.2 us (4%)
  starting transfers between devices  4.65 us (2%)
    reduce_scatter x1, waiting for transfers between devices, body(): summed = lax.psum_scatter(partial, 'head', scatter_dimension=1, tiled=True)  80 us
    all_gather x1, waiting for transfers between devices, body(): gathered = lax.all_gather(packed, ('span', 'head'), axis=0, tiled=False)  62.2 us
    pallas_call x1, Pallas kernels, attend(): pl.pallas_call(functools.partial(attend_kernel, spans=spans, neighbors=ne...  59 us
    pallas_call x2, Pallas kernels, grouped_matmul(): pl.pallas_call(matmul_kernel, out_shape=jax.ShapeDtypeStruct((rows, group...  28.9 us
    all_gather x1, blocking collectives, body(): every = lax.all_gather(lse, 'head', axis=0, tiled=False)  16.7 us
    all_to_all x1, blocking collectives, body(): lax.all_to_all(request, 'span', split_axis=0, concat_axis=0, tiled=True)  9.69 us
    pallas_call x1, Pallas kernels, project(): pl.pallas_call(project_kernel, out_shape=jax.ShapeDtypeStruct((rows, w.sh...  9.36 us
  transfers between devices with their start and end apart: 4, of which 2 were waited for; matrix products, arithmetic and copies ran while one was open for 5% of the time, Pallas kernels for 29%

profile of v1, /device:TPU:0, one launch (start us, length us, event | category | flops | bytes accessed | tf_op | source)
XLA Modules:
  0.0 302.0 jit_solution(8769610703854318957)
XLA Ops:
  6.5 1.6 fusion.1
  8.2 0.8 fusion.4
  9.0 0.1 copy.15
  9.1 0.1 reshape_squeeze.3
  9.3 0.1 broadcast_in_dim.14
  9.4 0.2 convert_reduce_fusion
  9.6 0.1 select_reduce_fusion
  9.8 9.7 %all_to_all.17 = s32[8,8,1]{1,2,0:T(1,128)S(1)} all-to-all(s32[8,8,1]{1,2,0:T(1,128)S(1)} %bitcast.21), channel_id=1, replica_groups=mesh['span'=8,'head'=4] {'span'}, dimensions={0} | all-to-all | bytes 512 | tf_op jit(solution)/shard_map/all_to_all | solution.py:194
  19.4 0.5 broadcast.29
  20.0 0.6 reduce.3
  20.7 5.0 %gather_fusion = bf16[64,32,1024]{2,1,0:T(8,128)(2,1)} fusion(bf16[64,32,1024]{2,1,0:T(8,128)(2,1)} %param.8, s32[1024]{0:T(1024)S(1)} %pad_clamp_fusion), kind=kCustom, calls=%fused_computation | custom fusion | bytes 8388864 | tf_op jit(solution)/shard_map/gather | solution.py:195
  25.8 4.6 %all-to-all-start.1 = ((bf16[64,32,1024]{2,1,0:T(8,128)(2,1)}), bf16[64,32,1024]{2,1,0:T(8,128)(2,1)}, u32[]{:S(2)}, u32[]{:S(2)}) async-start(bf16[64,32,1024]{2,1,0:T(8,128)(2,1)} %gather_fusion), calls=%async_computation.1 | async-start | bytes 8388608 | tf_op jit(solution)/shard_map/all_to_all | solution.py:196
  30.4 0.6 constant_dynamic-slice_fusion
  31.1 3.3 %slice.18 = bf16[1,1985,1024]{2,1,0:T(8,128)(2,1)S(1)} slice(bf16[1,2048,1024]{2,1,0:T(8,128)(2,1)} %bitcast.18), slice={[0:1], [63:2048], [0:1024]} | slice | bytes 8130560 | tf_op jit(solution)/shard_map/slice | solution.py:202
  34.4 2.4 pad_bitcast_fusion.x_ref
  36.8 62.2 %all-gather.7.cloned.1.call-done = bf16[4096,768]{1,0:T(8,128)(2,1)} async-done(((bf16[128,768]{1,0:T(8,128)(2,1)}), bf16[4096,768]{1,0:T(8,128)(2,1)}) %all-gather.7.cloned.1.call-update) | async-done | bytes 6291472 | tf_op jit(solution)/shard_map/all_gather | solution.py:176
  99.0 12.5 %shard_map.73.q_ref = bf16[2048,1024]{1,0:T(8,128)(2,1)} custom-call(bf16[2048,1024]{1,0:T(8,128)(2,1)} %pad_bitcast_fusion.x_ref, bf16[8,4,128,768]{3,2,1,0:T(8,128)(2,1)} %bitcast.22), custom_call_target="tpu_custom_call" | custom-call | flops 4294967296 | bytes 16777216 | tf_op jit(solution)/shard_map/pallas_call | solution.py:24
  111.5 16.4 %shard_map.74 = bf16[2048,2048]{1,0:T(8,128)(2,1)} custom-call(bf16[2048,1024]{1,0:T(8,128)(2,1)} %bitcast.5.x_ref, bf16[8,4,128,768]{3,2,1,0:T(8,128)(2,1)} %bitcast.23), custom_call_target="tpu_custom_call" | custom-call | flops 8589934592 | bytes 16777216 | tf_op jit(solution)/shard_map/pallas_call | solution.py:24
  127.9 59.0 %shard_map.75 = (bf16[2048,1024]{1,0:T(8,128)(2,1)}, f32[16,2048]{1,0:T(8,128)}) custom-call(s32[64]{0:T(128)} %copy-done.1, bf16[2048,1024]{1,0:T(8,128)(2,1)} %shard_map.73.q_ref, bf16[64,32,2048]{2,1,0:T(8,128)(2,1)} %bitcast.24), custom_call_target="tpu_custom_call" | custom-call | flops 8589934592 | bytes 16777216 | tf_op jit(solution)/shard_map/pallas_call | solution.py:94
  187.0 16.7 %all-gather.1 = f32[64,2048]{1,0:T(8,128)} all-gather(f32[16,2048]{1,0:T(8,128)} %get-tuple-element.8.own_ref), channel_id=3, replica_groups=mesh['span'=8,'head'=4] {'head'}, dimensions={0}, use_global_device_ids=true | all-gather | bytes 655360 | tf_op jit(solution)/shard_map/all_gather | solution.py:211
  203.6 9.4 %shard_map.76 = bf16[2048,1024]{1,0:T(8,128)(2,1)} custom-call(bf16[2048,1024]{1,0:T(8,128)(2,1)} %get-tuple-element.7.ctx_ref, f32[16,2048]{1,0:T(8,128)} %get-tuple-element.8.own_ref, f32[4,16,2048]{2,1,0:T(8,128)} %bitcast.19, bf16[1024,1024]{1,0:T(8,128)(2,1)} %all-gather.5.cloned.1.call-done.w_ref), custom_call_target="tpu_custom_call" | custom-call | tf_op jit(solution)/shard_map/pallas_call | solution.py:150
  213.0 80.0 %reduce-scatter.2.cloned.1.call-done = bf16[2048,256]{1,0:T(8,128)(2,1)} async-done(((bf16[2048,1024]{1,0:T(8,128)(2,1)}), bf16[2048,256]{1,0:T(8,128)(2,1)}) %reduce-scatter.2.cloned.1.call-update) | async-done | bytes 1048592 | tf_op jit(solution)/shard_map/reduce_scatter | solution.py:213
  293.0 1.3 slice.19
  294.3 1.2 pad_bitcast_fusion.1
  (18 shorter events, 0.5 us)
Async XLA Ops:
  6.5 23.9 %copy-start = (bf16[256,1024]{1,0:T(8,128)(2,1)S(1)}, bf16[256,1024]{1,0:T(8,128)(2,1)}, u32[]{:S(2)}) copy-start(bf16[256,1024]{1,0:T(8,128)(2,1)} %param.13) | copy-start | bytes 1572868
  6.5 92.5 %all-gather.7.cloned.1.call-start = ((), (), s32[]{:S(2)}) async-start(), calls=%async_computation.5 | async-start | bytes 6488064 | tf_op jit(solution)/shard_map/all_gather | solution.py:176
  9.6 16.2 %copy-start.1 = (s32[64]{0:T(128)}, s32[64]{0:T(128)S(1)}, u32[]{:S(2)}) copy-start(s32[64]{0:T(128)S(1)} %multiply_add_fusion.position_ref) | copy-start | bytes 772
  25.8 85.7 %all-to-all-start.1 = ((bf16[64,32,1024]{2,1,0:T(8,128)(2,1)}), bf16[64,32,1024]{2,1,0:T(8,128)(2,1)}, u32[]{:S(2)}, u32[]{:S(2)}) async-start(bf16[64,32,1024]{2,1,0:T(8,128)(2,1)} %gather_fusion), calls=%async_computation.1 | async-start | bytes 8388608 | tf_op jit(solution)/shard_map/all_to_all | solution.py:196
  30.3 173.3 %all-gather.5.cloned.1.call-start = ((), (), s32[]{:S(2)}) async-start(), calls=%async_computation.3 | async-start | bytes 2162688 | tf_op jit(solution)/shard_map/all_gather | solution.py:180
  31.1 261.9 %reduce-scatter.2.cloned.1.call-start = ((), (), s32[]{:S(2)}) async-start(), calls=%async_computation.4 | async-start | bytes 5242880 | tf_op jit(solution)/shard_map/reduce_scatter | solution.py:213
Sparse Core Ops, SparseCore 0:
  10.2 88.7 all-gather.6
  101.9 59.3 all-gather.4
  213.1 79.8 reduce-scatter.1

commit v2 on v1

v2 whole, which is shorter than its diff:
```python
import functools

import jax
import jax.numpy as jnp
from jax import lax
from jax.experimental import pallas as pl
from jax.experimental.pallas import tpu as pltpu
from jax.sharding import PartitionSpec as P

HEAD_DIM = 64
SPAN_LEN = 64
SEQ_LEN = 2048
VMEM = 56 * 1024 * 1024
CHUNKS = 2


def matmul_kernel(x_ref, w_ref, o_ref):
    groups = w_ref.shape[1]
    cols = w_ref.shape[3]
    x = x_ref[...]
    for g in range(groups):
        w = w_ref[:, g].reshape(x_ref.shape[1], cols)
        o_ref[:, g * cols : (g + 1) * cols] = jnp.dot(
            x, w, preferred_element_type=jnp.float32
        ).astype(o_ref.dtype)


def grouped_matmul(x, w, cols, col_block, tile):
    peers, groups, depth, _ = w.shape
    rows, width = x.shape
    return pl.pallas_call(
        matmul_kernel,
        out_shape=jax.ShapeDtypeStruct((rows, groups * cols), jnp.bfloat16),
        grid=(rows // tile,),
        in_specs=[
            pl.BlockSpec((tile, width), lambda i: (i, 0)),
            pl.BlockSpec((peers, groups, depth, cols), lambda i: (0, 0, 0, col_block)),
        ],
        out_specs=pl.BlockSpec((tile, groups * cols), lambda i: (i, 0)),
        compiler_params=pltpu.CompilerParams(vmem_limit_bytes=VMEM),
        cost_estimate=pl.CostEstimate(
            flops=2 * rows * width * groups * cols, bytes_accessed=16 << 20, transcendentals=0
        ),
    )(x, w)


def attend_kernel(position_ref, *refs, spans, neighbors, group_cols):
    kv_refs = refs[: spans * neighbors]
    q_ref, ctx_ref, lse_ref, top_ref, s_ref, e_ref = refs[spans * neighbors :]
    width = q_ref.shape[1]
    heads = width // HEAD_DIM
    groups = width // group_cols
    packed = group_cols // HEAD_DIM
    tokens = kv_refs[0].shape[1]
    keys = neighbors * tokens
    wide = packed * keys
    row_head = lax.broadcasted_iota(jnp.int32, (wide, group_cols), 0) // keys
    col_head = lax.broadcasted_iota(jnp.int32, (wide, group_cols), 1) // HEAD_DIM
    diagonal = row_head == col_head
    pair = 128 // keys
    lane_head = lax.broadcasted_iota(jnp.int32, (SPAN_LEN, 128), 1) // keys
    lane = lax.broadcasted_iota(jnp.int32, (SPAN_LEN, 128), 1)
    collect = (
        lax.broadcasted_iota(jnp.int32, (heads * keys, 128), 0) // keys
        == lax.broadcasted_iota(jnp.int32, (heads * keys, 128), 1)
    ).astype(jnp.bfloat16)

    def widened(c, base):
        part = jnp.concatenate(
            [kv_refs[c * neighbors + k][0, :, base : base + group_cols] for k in range(neighbors)],
            axis=0,
        )
        return jnp.where(diagonal, jnp.concatenate([part] * packed, axis=0), 0)

    for c in range(spans):
        row = slice(c * SPAN_LEN, (c + 1) * SPAN_LEN)
        for g in range(groups):
            s_ref[row, g * wide : (g + 1) * wide] = lax.dot_general(
                q_ref[row, g * group_cols : (g + 1) * group_cols],
                widened(c, g * 2 * group_cols),
                (((1,), (1,)), ((), ())),
                preferred_element_type=jnp.float32,
            ) * (HEAD_DIM ** (-0.5))
    tops = []
    for c in range(spans):
        row = slice(c * SPAN_LEN, (c + 1) * SPAN_LEN)
        top_all = jnp.zeros((SPAN_LEN, 128), jnp.float32)
        for t in range(heads // pair):
            s = s_ref[row, t * 128 : (t + 1) * 128]
            top = None
            for n in range(pair):
                m = jnp.max(
                    jnp.where(lane_head == n, s, -jnp.inf), axis=1, keepdims=True
                )
                top = m if top is None else jnp.where(lane_head == n, m, top)
                top_all = jnp.where(lane == t * pair + n, m, top_all)
            e_ref[row, t * 128 : (t + 1) * 128] = jnp.exp(s - top).astype(jnp.bfloat16)
        tops.append(top_all)
    top_all = jnp.concatenate(tops, axis=0)
    total = jnp.dot(e_ref[...], collect, preferred_element_type=jnp.float32)
    top_rows = top_all.T[:heads]
    top_ref[...] = top_rows
    lse_ref[...] = top_rows + jnp.log(total.T[:heads])
    for c in range(spans):
        row = slice(c * SPAN_LEN, (c + 1) * SPAN_LEN)
        for g in range(groups):
            ctx_ref[row, g * group_cols : (g + 1) * group_cols] = jnp.dot(
                e_ref[row, g * wide : (g + 1) * wide],
                widened(c, g * 2 * group_cols + group_cols),
                preferred_element_type=jnp.float32,
            ).astype(ctx_ref.dtype)


def attend(position, q, kv, first, span_count, neighbors, group_cols, spans=4):
    width = q.shape[1]
    rows = span_count * SPAN_LEN
    heads = width // HEAD_DIM
    _, tokens, wide = kv.shape
    score_cols = heads * neighbors * tokens
    begin = first // spans
    step_rows = spans * SPAN_LEN

    def neighbor_spec(j):
        return pl.BlockSpec(
            (1, tokens, wide),
            lambda i, p: (p[(i + begin) * (spans * neighbors) + j], 0, 0),
        )

    return pl.pallas_call(
        functools.partial(
            attend_kernel, spans=spans, neighbors=neighbors, group_cols=group_cols
        ),
        out_shape=(
            jax.ShapeDtypeStruct((rows, width), jnp.bfloat16),
            jax.ShapeDtypeStruct((heads, rows), jnp.float32),
            jax.ShapeDtypeStruct((heads, rows), jnp.float32),
        ),
        grid_spec=pltpu.PrefetchScalarGridSpec(
            num_scalar_prefetch=1,
            grid=(span_count // spans,),
            in_specs=[neighbor_spec(j) for j in range(spans * neighbors)]
            + [pl.BlockSpec((step_rows, width), lambda i, p: (i + begin, 0))],
            out_specs=[
                pl.BlockSpec((step_rows, width), lambda i, p: (i, 0)),
                pl.BlockSpec((heads, step_rows), lambda i, p: (0, i)),
                pl.BlockSpec((heads, step_rows), lambda i, p: (0, i)),
            ],
            scratch_shapes=[
                pltpu.VMEM((step_rows, score_cols), jnp.float32),
                pltpu.VMEM((step_rows, score_cols), jnp.bfloat16),
            ],
        ),
        compiler_params=pltpu.CompilerParams(vmem_limit_bytes=VMEM),
        cost_estimate=pl.CostEstimate(
            flops=span_count << 28, bytes_accessed=16 << 20, transcendentals=span_count << 16
        ),
    )(position, *([kv] * (spans * neighbors)), q)


def project_kernel(ctx_ref, own_ref, all_ref, w_ref, o_ref):
    every = all_ref[...]
    top = jnp.max(every, axis=0)
    total = jnp.sum(jnp.exp(every - top[None]), axis=0)
    scale = jnp.exp(own_ref[...] - top) / total
    high = scale.astype(jnp.bfloat16)
    low = (scale - high.astype(jnp.float32)).astype(jnp.bfloat16)
    heads = scale.shape[0]
    width = ctx_ref.shape[1]
    spread = (
        lax.broadcasted_iota(jnp.int32, (2 * heads, width), 0) % heads
        == lax.broadcasted_iota(jnp.int32, (2 * heads, width), 1) // HEAD_DIM
    ).astype(jnp.bfloat16)
    factor = lax.dot_general(
        jnp.concatenate([high, low], axis=0),
        spread,
        (((0,), (0,)), ((), ())),
        preferred_element_type=jnp.float32,
    )
    scaled = (ctx_ref[...].astype(jnp.float32) * factor).astype(jnp.bfloat16)
    o_ref[...] = jnp.dot(scaled, w_ref[...], preferred_element_type=jnp.float32).astype(
        o_ref.dtype
    )


def project(ctx, own, every, w, tile=256):
    rows, width = ctx.shape
    groups, heads, _ = every.shape
    return pl.pallas_call(
        project_kernel,
        out_shape=jax.ShapeDtypeStruct((rows, w.shape[1]), jnp.bfloat16),
        grid=(rows // tile,),
        in_specs=[
            pl.BlockSpec((tile, width), lambda i: (i, 0)),
            pl.BlockSpec((heads, tile), lambda i: (0, i)),
            pl.BlockSpec((groups, heads, tile), lambda i: (0, 0, i)),
            pl.BlockSpec(w.shape, lambda i: (0, 0)),
        ],
        out_specs=pl.BlockSpec((tile, w.shape[1]), lambda i: (i, 0)),
        compiler_params=pltpu.CompilerParams(vmem_limit_bytes=VMEM),
        cost_estimate=pl.CostEstimate(
            flops=2 * rows * width * w.shape[1], bytes_accessed=6 << 20, transcendentals=0
        ),
    )(ctx, own, every, w)


def body(
    decoder_states, encodings, neighbor_table, query_weight, key_weight, value_weight, out_weight
):
    peer_count = lax.axis_size("span")
    groups = lax.axis_size("head")
    model_width = decoder_states.shape[1]
    group_cols = query_weight.shape[1]
    me = lax.axis_index("span")
    packed = jnp.concatenate([key_weight, value_weight, query_weight], axis=1)
    part = model_width // peer_count
    packed = lax.dynamic_slice_in_dim(packed, me * part, part, 0)
    gathered = lax.all_gather(packed, ("span", "head"), axis=0, tiled=False)
    gathered = gathered.reshape(peer_count, groups, part, 3 * group_cols)
    out_part = group_cols // peer_count
    out_slice = lax.dynamic_slice_in_dim(out_weight, me * out_part, out_part, 0)
    out_all = lax.all_gather(out_slice, ("head", "span"), axis=0, tiled=True)

    shard_ids = neighbor_table[:, :, 0].reshape(-1)
    slot_ids = neighbor_table[:, :, 1].reshape(-1)
    entries = shard_ids.shape[0]
    per_peer = entries // peer_count
    numbering = jnp.arange(entries, dtype=jnp.int32)
    same_before = (shard_ids[:, None] == shard_ids[None, :]) & (
        numbering[None, :] < numbering[:, None]
    )
    ranking = jnp.sum(same_before.astype(jnp.int32), axis=1)
    position = shard_ids * per_peer + ranking
    placed = position[None, :] == numbering[:, None]
    request = jnp.sum(jnp.where(placed, slot_ids[None, :], 0), axis=1)
    wanted = lax.all_to_all(request, "span", split_axis=0, concat_axis=0, tiled=True)
    selected = encodings[wanted]
    arrived = lax.all_to_all(selected, "span", split_axis=0, concat_axis=0, tiled=True)

    sequences = decoder_states.shape[0] // SEQ_LEN
    offset = SPAN_LEN - 1
    states = decoder_states.reshape(sequences, SEQ_LEN, model_width)
    states = jnp.concatenate(
        [states[:, offset:], jnp.zeros((sequences, offset, model_width), states.dtype)], axis=1
    ).reshape(-1, model_width)
    tile = 512
    queries = grouped_matmul(states, gathered, group_cols, 2, tile)
    kv = grouped_matmul(arrived.reshape(-1, model_width), gathered, 2 * group_cols, 0, tile)
    kv = kv.reshape(entries, arrived.shape[1], -1)
    span_count, neighbors = neighbor_table.shape[:2]
    pieces = []
    chunk = span_count // CHUNKS
    for first in range(0, span_count, chunk):
        context, lse, top = attend(position, queries, kv, first, chunk, neighbors, group_cols)
        every = lax.all_gather(lse, "head", axis=0, tiled=False)
        partial = project(context, top, every, out_all)
        pieces.append(lax.psum_scatter(partial, "head", scatter_dimension=1, tiled=True))
    summed = jnp.concatenate(pieces, axis=0)
    summed = summed.reshape(sequences, SEQ_LEN, -1)
    summed = jnp.concatenate(
        [jnp.zeros((sequences, offset, summed.shape[2]), summed.dtype), summed[:, :-offset]], axis=1
    )
    return summed.reshape(decoder_states.shape[0], -1)


def solution(mesh):
    return jax.shard_map(
        body,
        mesh=mesh,
        in_specs=(
            P("span", None),
            P("span", "head", None),
            P("span", None, None),
            P(None, "head"),
            P(None, "head"),
            P(None, "head"),
            P("head", None),
        ),
        out_specs=P("span", "head"),
        check_vma=False,
    )
```

time: 303 us -> 270 us (0.89)
  Pallas kernels: 97.3 us -> 53.8 us
  blocking collectives: 26.4 us -> 41.9 us
  waiting for transfers between devices: 142 us -> 137 us
    pallas_call x1 -> x2, Pallas kernels: 59 us -> 19 us  [attend(): pl.pallas_call(functools.partial(attend_kernel, spans=spans, neighbors=ne...]
    reduce_scatter x1 -> x2, waiting for transfers between devices: 80 us -> 58.5 us  [body(): lax.psum_scatter(partial, 'head', scatter_dimension=1, tiled=True)]
    all_gather x1, waiting for transfers between devices: 0.01 us -> 16 us  [body(): out_all = lax.all_gather(out_slice, ('head', 'span'), axis=0, tiled=True)]
    all_gather x1 -> x2, blocking collectives: 16.7 us -> 32.2 us  [body(): every = lax.all_gather(lse, 'head', axis=0, tiled=False)]
    pallas_call x2, Pallas kernels: 28.9 us -> 21.6 us  [grouped_matmul(): pl.pallas_call(matmul_kernel, out_shape=jax.ShapeDtypeStruct((rows, group...]
    pallas_call x1 -> x2, Pallas kernels: 9.36 us -> 13.2 us  [project(): pl.pallas_call(project_kernel, out_shape=jax.ShapeDtypeStruct((rows, w.sh...]
  transfers between devices with their start and end apart: 4 -> 5, of which waited for: 2 -> 4; matrix products, arithmetic and copies ran while one was open for 5% -> 5% of each run, Pallas kernels for 29% -> 18%
where the time goes in v2:
time: 270 us; the launch traced here: 269 us
  waiting for transfers between devices  137 us (51%)
  Pallas kernels  53.8 us (20%)
  blocking collectives  41.9 us (16%)
  local copies, waits for them, and re-layouts  14.4 us (5%)
  between operations  13.2 us (5%)
  starting transfers between devices  4.68 us (2%)
  other arithmetic  3.85 us (1%)
    all_gather x1, waiting for transfers between devices, body(): gathered = lax.all_gather(packed, ('span', 'head'), axis=0, tiled=False)  62.2 us
    reduce_scatter x2, waiting for transfers between devices, body(): lax.psum_scatter(partial, 'head', scatter_dimension=1, tiled=True)  58.5 us
    all_gather x2, blocking collectives, body(): every = lax.all_gather(lse, 'head', axis=0, tiled=False)  32.2 us
    pallas_call x2, Pallas kernels, grouped_matmul(): pl.pallas_call(matmul_kernel, out_shape=jax.ShapeDtypeStruct((rows, group...  21.6 us
    pallas_call x2, Pallas kernels, attend(): pl.pallas_call(functools.partial(attend_kernel, spans=spans, neighbors=ne...  19 us
    all_gather x1, waiting for transfers between devices, body(): out_all = lax.all_gather(out_slice, ('head', 'span'), axis=0, tiled=True)  16 us
    pallas_call x2, Pallas kernels, project(): pl.pallas_call(project_kernel, out_shape=jax.ShapeDtypeStruct((rows, w.sh...  13.2 us
    all_to_all x1, blocking collectives, body(): lax.all_to_all(request, 'span', split_axis=0, concat_axis=0, tiled=True)  9.69 us
  transfers between devices with their start and end apart: 5, of which 4 were waited for; matrix products, arithmetic and copies ran while one was open for 5% of the time, Pallas kernels for 18%

profile of v2, /device:TPU:0, one launch (start us, length us, event | category | flops | bytes accessed | tf_op | source)
XLA Modules:
  0.0 268.7 jit_solution(7176519182142883579)
XLA Ops:
  6.5 1.6 fusion.1
  8.2 0.8 fusion.4
  9.8 9.7 %all_to_all.17 = s32[8,8,1]{1,2,0:T(1,128)S(1)} all-to-all(s32[8,8,1]{1,2,0:T(1,128)S(1)} %bitcast.39), channel_id=1, replica_groups=mesh['span'=8,'head'=4] {'span'}, dimensions={0} | all-to-all | bytes 512 | tf_op jit(solution)/shard_map/all_to_all | solution.py:235
  19.4 0.5 broadcast.29
  20.0 0.6 reduce.3
  20.7 5.0 %gather_fusion = bf16[64,32,1024]{2,1,0:T(8,128)(2,1)} fusion(bf16[64,32,1024]{2,1,0:T(8,128)(2,1)} %param.8, s32[1024]{0:T(1024)S(1)} %pad_clamp_fusion), kind=kCustom, calls=%fused_computation | custom fusion | bytes 8388864 | tf_op jit(solution)/shard_map/gather | solution.py:236
  25.8 4.5 %all-to-all-start.1 = ((bf16[64,32,1024]{2,1,0:T(8,128)(2,1)}), bf16[64,32,1024]{2,1,0:T(8,128)(2,1)}, u32[]{:S(2)}, u32[]{:S(2)}) async-start(bf16[64,32,1024]{2,1,0:T(8,128)(2,1)} %gather_fusion), calls=%async_computation.1 | async-start | bytes 8388608 | tf_op jit(solution)/shard_map/all_to_all | solution.py:237
  30.4 0.6 constant_dynamic-slice_fusion
  31.1 3.3 %slice.18 = bf16[1,1985,1024]{2,1,0:T(8,128)(2,1)S(1)} slice(bf16[1,2048,1024]{2,1,0:T(8,128)(2,1)} %bitcast.36), slice={[0:1], [63:2048], [0:1024]} | slice | bytes 8130560 | tf_op jit(solution)/shard_map/slice | solution.py:243
  34.4 2.4 pad_bitcast_fusion.x_ref
  36.8 62.2 %all-gather.8.cloned.1.call-done = bf16[4096,768]{1,0:T(8,128)(2,1)} async-done(((bf16[128,768]{1,0:T(8,128)(2,1)}), bf16[4096,768]{1,0:T(8,128)(2,1)}) %all-gather.8.cloned.1.call-update) | async-done | bytes 6291472 | tf_op jit(solution)/shard_map/all_gather | solution.py:217
  99.0 8.4 %shard_map.74.refs_8_ = bf16[2048,1024]{1,0:T(8,128)(2,1)} custom-call(bf16[2048,1024]{1,0:T(8,128)(2,1)} %pad_bitcast_fusion.x_ref, bf16[8,4,128,768]{3,2,1,0:T(8,128)(2,1)} %bitcast.40), custom_call_target="tpu_custom_call" | custom-call | flops 4294967296 | bytes 16777216 | tf_op jit(solution)/shard_map/pallas_call | solution.py:31
  107.4 13.2 %shard_map.73 = bf16[2048,2048]{1,0:T(8,128)(2,1)} custom-call(bf16[2048,1024]{1,0:T(8,128)(2,1)} %bitcast.2.x_ref, bf16[8,4,128,768]{3,2,1,0:T(8,128)(2,1)} %bitcast.41), custom_call_target="tpu_custom_call" | custom-call | flops 8589934592 | bytes 16777216 | tf_op jit(solution)/shard_map/pallas_call | solution.py:31
  120.6 9.4 %shard_map.75 = (bf16[1024,1024]{1,0:T(8,128)(2,1)}, f32[16,1024]{1,0:T(8,128)}, f32[16,1024]{1,0:T(8,128)}) custom-call(s32[64]{0:T(128)} %copy-done.1, bf16[64,32,2048]{2,1,0:T(8,128)(2,1)} %bitcast.20, bf16[64,32,2048]{2,1,0:T(8,128)(2,1)} %bitcast.21, bf16[64,32,2048]{2,1,0:T(8,128)(2,1)} %bitcast.22, bf16[64,32,2048]{2,1,0:T(8,128)(2,1)} %bitcast.23, ...), custom_call_target="tpu_custom_call" | custom-call | flops 4294967296 | bytes 16777216 | tf_op jit(solution)/shard_map/pallas_call | solution.py:129
  130.0 15.2 %all-gather.1 = f32[64,1024]{1,0:T(8,128)} all-gather(f32[16,1024]{1,0:T(8,128)} %get-tuple-element.13), channel_id=3, replica_groups=mesh['span'=8,'head'=4] {'head'}, dimensions={0}, use_global_device_ids=true | all-gather | bytes 327680 | tf_op jit(solution)/shard_map/all_gather | solution.py:254
  145.2 16.0 %all-gather.6.cloned.1.call-done.w_ref = bf16[1024,1024]{1,0:T(8,128)(2,1)} async-done(((bf16[32,1024]{1,0:T(8,128)(2,1)}), bf16[1024,1024]{1,0:T(8,128)(2,1)}) %all-gather.6.cloned.1.call-update) | async-done | bytes 2097168 | tf_op jit(solution)/shard_map/all_gather | solution.py:221
  161.2 6.6 %shard_map.76 = bf16[1024,1024]{1,0:T(8,128)(2,1)} custom-call(bf16[1024,1024]{1,0:T(8,128)(2,1)} %get-tuple-element.11.ctx_ref, f32[16,1024]{1,0:T(8,128)} %get-tuple-element.12.own_ref, f32[4,16,1024]{2,1,0:T(8,128)} %bitcast.37, bf16[1024,1024]{1,0:T(8,128)(2,1)} %all-gather.6.cloned.1.call-done.w_ref), custom_call_target="tpu_custom_call" | custom-call | flops 2147483648 | bytes 6291456 | tf_op jit(solution)/shard_map/pallas_call | solution.py:188
  167.8 9.6 %shard_map.77 = (bf16[1024,1024]{1,0:T(8,128)(2,1)}, f32[16,1024]{1,0:T(8,128)}, f32[16,1024]{1,0:T(8,128)}) custom-call(s32[64]{0:T(128)} %copy-done.1, bf16[64,32,2048]{2,1,0:T(8,128)(2,1)} %bitcast.28, bf16[64,32,2048]{2,1,0:T(8,128)(2,1)} %bitcast.29, bf16[64,32,2048]{2,1,0:T(8,128)(2,1)} %bitcast.30, bf16[64,32,2048]{2,1,0:T(8,128)(2,1)} %bitcast.31, ...), custom_call_target="tpu_custom_call" | custom-call | flops 4294967296 | bytes 16777216 | tf_op jit(solution)/shard_map/pallas_call | solution.py:129
  177.4 17.1 %all-gather.2 = f32[64,1024]{1,0:T(8,128)} all-gather(f32[16,1024]{1,0:T(8,128)} %get-tuple-element.16), channel_id=4, replica_groups=mesh['span'=8,'head'=4] {'head'}, dimensions={0}, use_global_device_ids=true | all-gather | bytes 327680 | tf_op jit(solution)/shard_map/all_gather | solution.py:254
  194.5 6.6 %shard_map.78 = bf16[1024,1024]{1,0:T(8,128)(2,1)} custom-call(bf16[1024,1024]{1,0:T(8,128)(2,1)} %get-tuple-element.14.ctx_ref, f32[16,1024]{1,0:T(8,128)} %get-tuple-element.15.own_ref, f32[4,16,1024]{2,1,0:T(8,128)} %bitcast.38, bf16[1024,1024]{1,0:T(8,128)(2,1)} %all-gather.6.cloned.1.call-done.w_ref), custom_call_target="tpu_custom_call" | custom-call | flops 2147483648 | bytes 6291456 | tf_op jit(solution)/shard_map/pallas_call | solution.py:188
  201.1 13.5 %reduce-scatter.3.cloned.1.call-done = bf16[1024,256]{1,0:T(8,128)(2,1)} async-done(((bf16[1024,1024]{1,0:T(8,128)(2,1)}), bf16[1024,256]{1,0:T(8,128)(2,1)}) %reduce-scatter.3.cloned.1.call-update) | async-done | bytes 524304 | tf_op jit(solution)/shard_map/reduce_scatter | solution.py:256
  214.7 45.0 %reduce-scatter.5.cloned.1.call-done = bf16[1024,256]{1,0:T(8,128)(2,1)} async-done(((bf16[1024,1024]{1,0:T(8,128)(2,1)}), bf16[1024,256]{1,0:T(8,128)(2,1)}) %reduce-scatter.5.cloned.1.call-update) | async-done | bytes 524304 | tf_op jit(solution)/shard_map/reduce_scatter | solution.py:256
  259.7 1.3 maximum_bitcast_fusion
  261.0 1.2 pad_bitcast_fusion.1
  (25 shorter events, 1.1 us)
Async XLA Ops:
  6.5 23.8 %copy-start = (bf16[256,1024]{1,0:T(8,128)(2,1)S(1)}, bf16[256,1024]{1,0:T(8,128)(2,1)}, u32[]{:S(2)}) copy-start(bf16[256,1024]{1,0:T(8,128)(2,1)} %param.13) | copy-start | bytes 1572868
  6.5 92.4 %all-gather.8.cloned.1.call-start = ((), (), s32[]{:S(2)}) async-start(), calls=%async_computation.7 | async-start | bytes 6488064 | tf_op jit(solution)/shard_map/all_gather | solution.py:217
  9.6 16.2 %copy-start.1 = (s32[64]{0:T(128)}, s32[64]{0:T(128)S(1)}, u32[]{:S(2)}) copy-start(s32[64]{0:T(128)S(1)} %multiply_add_fusion.position_ref) | copy-start | bytes 772
  25.8 81.6 %all-to-all-start.1 = ((bf16[64,32,1024]{2,1,0:T(8,128)(2,1)}), bf16[64,32,1024]{2,1,0:T(8,128)(2,1)}, u32[]{:S(2)}, u32[]{:S(2)}) async-start(bf16[64,32,1024]{2,1,0:T(8,128)(2,1)} %gather_fusion), calls=%async_computation.1 | async-start | bytes 8388608 | tf_op jit(solution)/shard_map/all_to_all | solution.py:237
  30.3 130.8 %all-gather.6.cloned.1.call-start = ((), (), s32[]{:S(2)}) async-start(), calls=%async_computation.4 | async-start | bytes 2162688 | tf_op jit(solution)/shard_map/all_gather | solution.py:221
  31.1 183.6 %reduce-scatter.3.cloned.1.call-start = ((), (), s32[]{:S(2)}) async-start(), calls=%async_computation.5 | async-start | bytes 2621440 | tf_op jit(solution)/shard_map/reduce_scatter | solution.py:256
  167.8 91.9 %reduce-scatter.5.cloned.1.call-start = ((), (), s32[]{:S(2)}) async-start(), calls=%async_computation.6 | async-start | bytes 2621440 | tf_op jit(solution)/shard_map/reduce_scatter | solution.py:256
Sparse Core Ops, SparseCore 0:
  10.2 88.7 all-gather.7
  101.8 59.2 all-gather.5
  167.9 46.7 reduce-scatter.2
  216.8 42.8 reduce-scatter.4

commit v3 on v2

--- a/solution.py
+++ b/solution.py
@@ -216,10 +216,6 @@
     packed = lax.dynamic_slice_in_dim(packed, me * part, part, 0)
     gathered = lax.all_gather(packed, ("span", "head"), axis=0, tiled=False)
     gathered = gathered.reshape(peer_count, groups, part, 3 * group_cols)
-    out_part = group_cols // peer_count
-    out_slice = lax.dynamic_slice_in_dim(out_weight, me * out_part, out_part, 0)
-    out_all = lax.all_gather(out_slice, ("head", "span"), axis=0, tiled=True)
-
     shard_ids = neighbor_table[:, :, 0].reshape(-1)
     slot_ids = neighbor_table[:, :, 1].reshape(-1)
     entries = shard_ids.shape[0]
@@ -233,6 +229,8 @@
     placed = position[None, :] == numbering[:, None]
     request = jnp.sum(jnp.where(placed, slot_ids[None, :], 0), axis=1)
     wanted = lax.all_to_all(request, "span", split_axis=0, concat_axis=0, tiled=True)
+    wanted, late_out = lax.optimization_barrier((wanted, out_weight))
+    out_all = lax.all_gather(late_out, "head", axis=0, tiled=True)
     selected = encodings[wanted]
     arrived = lax.all_to_all(selected, "span", split_axis=0, concat_axis=0, tiled=True)
 

time: 270 us -> 262 us (0.970)
  waiting for transfers between devices: 137 us -> 127 us
    all_gather x1, waiting for transfers between devices: 16 us -> 6.23 us  [body(): out_all = lax.all_gather(late_out, 'head', axis=0, tiled=True)]
where the time goes in v3:
time: 262 us; the launch traced here: 261 us
  waiting for transfers between devices  127 us (48%)
  Pallas kernels  53.8 us (21%)
  blocking collectives  44.3 us (17%)
  local copies, waits for them, and re-layouts  13.8 us (5%)
  between operations  13.2 us (5%)
  starting transfers between devices  4.68 us (2%)
  other arithmetic  3.78 us (1%)
    all_gather x1, waiting for transfers between devices, body(): gathered = lax.all_gather(packed, ('span', 'head'), axis=0, tiled=False)  62.2 us
    reduce_scatter x2, waiting for transfers between devices, body(): lax.psum_scatter(partial, 'head', scatter_dimension=1, tiled=True)  58.2 us
    all_gather x2, blocking collectives, body(): every = lax.all_gather(lse, 'head', axis=0, tiled=False)  34.6 us
    pallas_call x2, Pallas kernels, grouped_matmul(): pl.pallas_call(matmul_kernel, out_shape=jax.ShapeDtypeStruct((rows, group...  21.7 us
    pallas_call x2, Pallas kernels, attend(): pl.pallas_call(functools.partial(attend_kernel, spans=spans, neighbors=ne...  18.9 us
    pallas_call x2, Pallas kernels, project(): pl.pallas_call(project_kernel, out_shape=jax.ShapeDtypeStruct((rows, w.sh...  13.2 us
    all_to_all x1, blocking collectives, body(): lax.all_to_all(request, 'span', split_axis=0, concat_axis=0, tiled=True)  9.69 us
    all_gather x1, waiting for transfers between devices, body(): out_all = lax.all_gather(late_out, 'head', axis=0, tiled=True)  6.23 us
  transfers between devices with their start and end apart: 5, of which 4 were waited for; matrix products, arithmetic and copies ran while one was open for 5% of the time, Pallas kernels for 18%

profile of v3, /device:TPU:0, one launch (start us, length us, event | category | flops | bytes accessed | tf_op | source)
XLA Modules:
  0.0 261.0 jit_solution(10480377056315314342)
XLA Ops:
  6.5 1.6 fusion.1
  8.2 0.8 fusion.3
  9.7 9.7 %all_to_all.17 = s32[8,8,1]{1,2,0:T(1,128)S(1)} all-to-all(s32[8,8,1]{1,2,0:T(1,128)S(1)} %bitcast.37), channel_id=1, replica_groups=mesh['span'=8,'head'=4] {'span'}, dimensions={0} | all-to-all | bytes 512 | tf_op jit(solution)/shard_map/all_to_all | solution.py:231
  19.4 0.5 broadcast.15
  19.9 0.6 reduce.3
  20.7 5.1 %gather_fusion = bf16[64,32,1024]{2,1,0:T(8,128)(2,1)} fusion(bf16[64,32,1024]{2,1,0:T(8,128)(2,1)} %param.8, s32[1024]{0:T(1024)S(1)} %pad_clamp_fusion), kind=kCustom, calls=%fused_computation | custom fusion | bytes 8388864 | tf_op jit(solution)/shard_map/gather | solution.py:234
  25.7 4.6 %all-to-all-start.1 = ((bf16[64,32,1024]{2,1,0:T(8,128)(2,1)}), bf16[64,32,1024]{2,1,0:T(8,128)(2,1)}, u32[]{:S(2)}, u32[]{:S(2)}) async-start(bf16[64,32,1024]{2,1,0:T(8,128)(2,1)} %gather_fusion), calls=%async_computation.1 | async-start | bytes 8388608 | tf_op jit(solution)/shard_map/all_to_all | solution.py:235
  30.3 0.7 all-gather.6.cloned.1.call-update
  31.1 3.3 %slice.18 = bf16[1,1985,1024]{2,1,0:T(8,128)(2,1)S(1)} slice(bf16[1,2048,1024]{2,1,0:T(8,128)(2,1)} %bitcast.34), slice={[0:1], [63:2048], [0:1024]} | slice | bytes 8130560 | tf_op jit(solution)/shard_map/slice | solution.py:241
  34.3 2.4 pad_bitcast_fusion.x_ref
  36.7 62.2 %all-gather.8.cloned.1.call-done = bf16[4096,768]{1,0:T(8,128)(2,1)} async-done(((bf16[128,768]{1,0:T(8,128)(2,1)}), bf16[4096,768]{1,0:T(8,128)(2,1)}) %all-gather.8.cloned.1.call-update) | async-done | bytes 6291472 | tf_op jit(solution)/shard_map/all_gather | solution.py:217
  98.9 8.4 %shard_map.74.refs_8_ = bf16[2048,1024]{1,0:T(8,128)(2,1)} custom-call(bf16[2048,1024]{1,0:T(8,128)(2,1)} %pad_bitcast_fusion.x_ref, bf16[8,4,128,768]{3,2,1,0:T(8,128)(2,1)} %bitcast.38), custom_call_target="tpu_custom_call" | custom-call | flops 4294967296 | bytes 16777216 | tf_op jit(solution)/shard_map/pallas_call | solution.py:31
  107.3 13.3 %shard_map.73 = bf16[2048,2048]{1,0:T(8,128)(2,1)} custom-call(bf16[2048,1024]{1,0:T(8,128)(2,1)} %bitcast.1.x_ref, bf16[8,4,128,768]{3,2,1,0:T(8,128)(2,1)} %bitcast.39), custom_call_target="tpu_custom_call" | custom-call | flops 8589934592 | bytes 16777216 | tf_op jit(solution)/shard_map/pallas_call | solution.py:31
  120.6 9.4 %shard_map.75 = (bf16[1024,1024]{1,0:T(8,128)(2,1)}, f32[16,1024]{1,0:T(8,128)}, f32[16,1024]{1,0:T(8,128)}) custom-call(s32[64]{0:T(128)} %copy-done, bf16[64,32,2048]{2,1,0:T(8,128)(2,1)} %bitcast.18, bf16[64,32,2048]{2,1,0:T(8,128)(2,1)} %bitcast.19, bf16[64,32,2048]{2,1,0:T(8,128)(2,1)} %bitcast.20, bf16[64,32,2048]{2,1,0:T(8,128)(2,1)} %bitcast.21, ...), custom_call_target="tpu_custom_call" | custom-call | flops 4294967296 | bytes 16777216 | tf_op jit(solution)/shard_map/pallas_call | solution.py:129
  129.9 17.3 %all-gather.1 = f32[64,1024]{1,0:T(8,128)} all-gather(f32[16,1024]{1,0:T(8,128)} %get-tuple-element.16), channel_id=3, replica_groups=mesh['span'=8,'head'=4] {'head'}, dimensions={0}, use_global_device_ids=true | all-gather | bytes 327680 | tf_op jit(solution)/shard_map/all_gather | solution.py:252
  147.3 6.2 %all-gather.6.cloned.1.call-done.w_ref = bf16[1024,1024]{1,0:T(8,128)(2,1)} async-done(((bf16[256,1024]{1,0:T(8,128)(2,1)}), bf16[1024,1024]{1,0:T(8,128)(2,1)}) %all-gather.6.cloned.1.call-update) | async-done | bytes 2097168 | tf_op jit(solution)/shard_map/all_gather | solution.py:233
  153.5 6.6 %shard_map.76 = bf16[1024,1024]{1,0:T(8,128)(2,1)} custom-call(bf16[1024,1024]{1,0:T(8,128)(2,1)} %get-tuple-element.14.ctx_ref, f32[16,1024]{1,0:T(8,128)} %get-tuple-element.15.own_ref, f32[4,16,1024]{2,1,0:T(8,128)} %bitcast.35, bf16[1024,1024]{1,0:T(8,128)(2,1)} %all-gather.6.cloned.1.call-done.w_ref), custom_call_target="tpu_custom_call" | custom-call | flops 2147483648 | bytes 6291456 | tf_op jit(solution)/shard_map/pallas_call | solution.py:188
  160.1 9.6 %shard_map.77 = (bf16[1024,1024]{1,0:T(8,128)(2,1)}, f32[16,1024]{1,0:T(8,128)}, f32[16,1024]{1,0:T(8,128)}) custom-call(s32[64]{0:T(128)} %copy-done, bf16[64,32,2048]{2,1,0:T(8,128)(2,1)} %bitcast.26, bf16[64,32,2048]{2,1,0:T(8,128)(2,1)} %bitcast.27, bf16[64,32,2048]{2,1,0:T(8,128)(2,1)} %bitcast.28, bf16[64,32,2048]{2,1,0:T(8,128)(2,1)} %bitcast.29, ...), custom_call_target="tpu_custom_call" | custom-call | flops 4294967296 | bytes 16777216 | tf_op jit(solution)/shard_map/pallas_call | solution.py:129
  169.7 17.3 %all-gather.2 = f32[64,1024]{1,0:T(8,128)} all-gather(f32[16,1024]{1,0:T(8,128)} %get-tuple-element.20), channel_id=4, replica_groups=mesh['span'=8,'head'=4] {'head'}, dimensions={0}, use_global_device_ids=true | all-gather | bytes 327680 | tf_op jit(solution)/shard_map/all_gather | solution.py:252
  187.1 6.6 %shard_map.78 = bf16[1024,1024]{1,0:T(8,128)(2,1)} custom-call(bf16[1024,1024]{1,0:T(8,128)(2,1)} %get-tuple-element.18.ctx_ref, f32[16,1024]{1,0:T(8,128)} %get-tuple-element.19.own_ref, f32[4,16,1024]{2,1,0:T(8,128)} %bitcast.36, bf16[1024,1024]{1,0:T(8,128)(2,1)} %all-gather.6.cloned.1.call-done.w_ref), custom_call_target="tpu_custom_call" | custom-call | flops 2147483648 | bytes 6291456 | tf_op jit(solution)/shard_map/pallas_call | solution.py:188
  193.7 13.2 %reduce-scatter.3.cloned.1.call-done = bf16[1024,256]{1,0:T(8,128)(2,1)} async-done(((bf16[1024,1024]{1,0:T(8,128)(2,1)}), bf16[1024,256]{1,0:T(8,128)(2,1)}) %reduce-scatter.3.cloned.1.call-update) | async-done | bytes 524304 | tf_op jit(solution)/shard_map/reduce_scatter | solution.py:254
  206.9 45.0 %reduce-scatter.5.cloned.1.call-done = bf16[1024,256]{1,0:T(8,128)(2,1)} async-done(((bf16[1024,1024]{1,0:T(8,128)(2,1)}), bf16[1024,256]{1,0:T(8,128)(2,1)}) %reduce-scatter.5.cloned.1.call-update) | async-done | bytes 524304 | tf_op jit(solution)/shard_map/reduce_scatter | solution.py:254
  251.9 1.3 maximum_bitcast_fusion
  253.3 1.2 pad_bitcast_fusion.1
  (22 shorter events, 1.1 us)
Async XLA Ops:
  6.5 92.4 %all-gather.8.cloned.1.call-start = ((), (), s32[]{:S(2)}) async-start(), calls=%async_computation.7 | async-start | bytes 6488064 | tf_op jit(solution)/shard_map/all_gather | solution.py:217
  9.5 16.2 %copy-start = (s32[64]{0:T(128)}, s32[64]{0:T(128)S(1)}, u32[]{:S(2)}) copy-start(s32[64]{0:T(128)S(1)} %multiply_add_fusion.position_ref) | copy-start | bytes 772
  25.7 81.6 %all-to-all-start.1 = ((bf16[64,32,1024]{2,1,0:T(8,128)(2,1)}), bf16[64,32,1024]{2,1,0:T(8,128)(2,1)}, u32[]{:S(2)}, u32[]{:S(2)}) async-start(bf16[64,32,1024]{2,1,0:T(8,128)(2,1)} %gather_fusion), calls=%async_computation.1 | async-start | bytes 8388608 | tf_op jit(solution)/shard_map/all_to_all | solution.py:235
  30.3 123.2 %all-gather.6.cloned.1.call-start = ((), (), s32[]{:S(2)}) async-start(), calls=%async_computation.4 | async-start | bytes 2621440 | tf_op jit(solution)/shard_map/all_gather | solution.py:233
  31.0 175.9 %reduce-scatter.3.cloned.1.call-start = ((), (), s32[]{:S(2)}) async-start(), calls=%async_computation.5 | async-start | bytes 2621440 | tf_op jit(solution)/shard_map/reduce_scatter | solution.py:254
  160.1 91.8 %reduce-scatter.5.cloned.1.call-start = ((), (), s32[]{:S(2)}) async-start(), calls=%async_computation.6 | async-start | bytes 2621440 | tf_op jit(solution)/shard_map/reduce_scatter | solution.py:254
Sparse Core Ops, SparseCore 0:
  10.2 88.6 all-gather.7
  100.5 52.9 all-gather.5
  160.2 46.6 reduce-scatter.2
  209.1 42.8 reduce-scatter.4
